TPU v7x, 32 devices: a whole 2x2x4 slice. The times are simulated.
32 devices in a mesh: kpt: 2 (over y), ga: 16 (over z, x, core).
Axes of the slice: x: 2, y: 2, z: 4, core: 2. Of those that a mesh axis runs over, the one named last changes fastest.
Arguments:
- miller_index: int32 [3, 12288], P(None, 'ga'), may hold values from -12 to 12
- kpoint: float32 [6], P('kpt'), parts along dimension 0, may hold values from -0.5 to 0.5
- waves: bfloat16 [2, 256, 12288], P(None, 'kpt', 'ga'), parts along dimension 1, may hold values from -6 to 6
- species: int32 [16], replicated, may hold values from 0 to 3
- counts: int32 [16], replicated, may hold values from 1 to 8
- positions: int32 [3, 16], replicated, may hold values from 0 to 63
- radial_coef: float32 [4, 8, 16], replicated, may hold values from -4 to 4
- coupling: float32 [16, 8, 8], replicated, as said below
Outputs:
- applied: bfloat16 [2, 256, 12288], P(None, 'kpt', 'ga'), parts along dimension 1
- energy: float32 [256], P('kpt'), parts along dimension 0
There are 2 independent parts, one for each index of `kpt`. A program takes and returns all parts, laid end to end along the dimension named above; an argument that names none is the same for every part. Nothing has to cross between parts.
Inputs may be any that keep to these rules, and one draw needn't show every extreme that they name: `coupling`: symmetric in its last two dimensions.
All inputs are finite; a program needn't handle non-finite values.
Results may differ from a plain program's by a relative error of at most 0.0062.
Values may be sent and summed in bfloat16 or wider, within the bound.
A program may use at most 64 MiB of HBM per device.

v0:
```python
import math
import jax
import jax.numpy as jnp
from jax import lax
from jax.sharding import PartitionSpec as P

PROJ = 8
MGRID = 64
ATOM_BLOCK = 16


def prepare(miller_index, kpoint, terms):
    shifted = miller_index.astype(jnp.float32) + kpoint[:, None]
    squared = jnp.sum(shifted * shifted, axis=0)
    widths = 0.001 * 1.5 ** jnp.arange(terms).astype(jnp.float32)
    basis = jnp.exp(-widths[:, None] * squared[None, :])
    angular = jnp.concatenate(
        [jnp.ones_like(squared)[None], shifted / jnp.sqrt(squared + 1.0)[None]], 0
    )
    angular = jnp.concatenate([angular, angular], 0)
    return (basis, angular)


def projectors(
    first, miller_index, kpoint, basis, angular, species, counts, positions, radial_coef, scaling
):
    kinds = lax.dynamic_slice_in_dim(species, first, ATOM_BLOCK)
    numbers = lax.dynamic_slice_in_dim(counts, first, ATOM_BLOCK)
    places = lax.dynamic_slice_in_dim(positions, first, ATOM_BLOCK, 1)
    selector = (kinds[:, None] == jnp.arange(radial_coef.shape[0])[None, :]).astype(jnp.float32)
    chosen = jnp.einsum("as,sjr->ajr", selector, radial_coef, precision=lax.Precision.HIGHEST)
    radial = jnp.einsum("ajr,rg->ajg", chosen, basis, precision=lax.Precision.HIGHEST)
    active = (jnp.arange(PROJ)[None, :] < numbers[:, None]).astype(jnp.float32)
    amplitude = radial * angular[None] * active[:, :, None] * scaling
    winding = jnp.mod(jnp.sum(miller_index[:, None, :] * places[:, :, None], axis=0), MGRID)
    offset = jnp.sum(kpoint[:, None] * places.astype(jnp.float32), axis=0)
    phase = 2.0 * math.pi / MGRID * (winding.astype(jnp.float32) + offset[:, None])
    planes = miller_index.shape[1]
    real_part = (
        (amplitude * jnp.cos(phase)[:, None, :])
        .astype(jnp.bfloat16)
        .reshape(ATOM_BLOCK * PROJ, planes)
    )
    imag_part = (
        (-amplitude * jnp.sin(phase)[:, None, :])
        .astype(jnp.bfloat16)
        .reshape(ATOM_BLOCK * PROJ, planes)
    )
    return (real_part, imag_part)


def measure(real_part, imag_part, coeffs):
    over_re = jnp.einsum(
        "sg,bg->sb", real_part, coeffs[0], preferred_element_type=jnp.float32
    ) + jnp.einsum("sg,bg->sb", imag_part, coeffs[1], preferred_element_type=jnp.float32)
    over_im = jnp.einsum(
        "sg,bg->sb", real_part, coeffs[1], preferred_element_type=jnp.float32
    ) - jnp.einsum("sg,bg->sb", imag_part, coeffs[0], preferred_element_type=jnp.float32)
    return jnp.stack([over_re, over_im])


def spread(rows, real_part, imag_part):
    out_re = jnp.einsum(
        "sb,sg->bg", rows[0], real_part, preferred_element_type=jnp.float32
    ) - jnp.einsum("sb,sg->bg", rows[1], imag_part, preferred_element_type=jnp.float32)
    out_im = jnp.einsum(
        "sb,sg->bg", rows[1], real_part, preferred_element_type=jnp.float32
    ) + jnp.einsum("sb,sg->bg", rows[0], imag_part, preferred_element_type=jnp.float32)
    return jnp.stack([out_re, out_im])


def on_device(miller_index, kpoint, waves, species, counts, positions, radial_coef, coupling):
    planes = waves.shape[2]
    bands = waves.shape[1]
    scaling = 1.0 / math.sqrt(planes * lax.axis_size("ga"))
    atoms = coupling.shape[0]
    slots_all = atoms * PROJ
    blocks = atoms // ATOM_BLOCK
    width = ATOM_BLOCK * PROJ
    basis, angular = prepare(miller_index, kpoint, radial_coef.shape[2])

    def build(index):
        return projectors(
            index * ATOM_BLOCK,
            miller_index,
            kpoint,
            basis,
            angular,
            species,
            counts,
            positions,
            radial_coef,
            scaling,
        )

    empty = jnp.zeros((2, bands, planes), jnp.float32)

    def first_pass(index, table):
        real_part, imag_part = build(index)
        return lax.dynamic_update_slice_in_dim(
            table, measure(real_part, imag_part, waves), index * width, 1
        )

    local = lax.fori_loop(0, blocks, first_pass, jnp.zeros((2, slots_all, bands), jnp.float32))
    summed = lax.psum(local, "ga")
    shaped = summed.reshape(2, atoms, PROJ, summed.shape[2])
    weighted = jnp.einsum("aij,cajb->caib", coupling, shaped, precision=lax.Precision.HIGHEST)
    weighted = weighted.reshape(2, atoms * PROJ, summed.shape[2])
    energy = jnp.sum(summed * weighted, axis=(0, 1))
    table = weighted.astype(jnp.bfloat16)

    def second_pass(index, output):
        real_part, imag_part = build(index)
        rows = lax.dynamic_slice_in_dim(table, index * width, width, 1)
        return output + spread(rows, real_part, imag_part)

    output = lax.fori_loop(0, blocks, second_pass, empty)
    return (output.astype(jnp.bfloat16), energy / slots_all)


def solution(mesh):
    in_specs = (P(None, "ga"), P("kpt"), P(None, "kpt", "ga"), P(), P(), P(), P(), P())
    out_specs = (P(None, "kpt", "ga"), P("kpt"))
    return jax.shard_map(
        on_device, mesh=mesh, in_specs=in_specs, out_specs=out_specs, check_vma=False
    )
```

profile of v0, /device:TPU:8, one launch (start us, length us, event | category | flops | bytes accessed | tf_op | source)
XLA Modules:
  0.0 116.9 jit_solution(3049479459820801523)
XLA Ops:
  7.3 0.6 copy-done.6
  7.8 0.8 multiply_reduce_fusion.2
  8.6 0.8 multiply_reduce_fusion.1
  9.6 0.6 copy-done.8
  10.3 0.3 fusion.40
  10.6 0.4 copy-done.7
  10.9 0.2 fusion.33
  11.2 0.6 fusion.8
  11.8 0.4 copy-done.1
  12.2 0.2 fusion.9
  12.4 0.2 fusion.13
  12.6 0.2 fusion.5
  12.8 0.2 fusion.6
  13.1 0.7 pad_maximum_fusion.1
  13.8 0.7 copy-done.4
  14.6 91.3 %all-reduce.2.cloned.1.call-done = f32[2,128,128]{2,1,0:T(8,128)} async-done(((f32[2,128,128]{2,1,0:T(8,128)}), f32[2,128,128]{2,1,0:T(8,128)}) %all-reduce.2.cloned.1.call-update) | async-done | bytes 131088 | tf_op jit(solution)/shard_map/psum | solution.py:105
  105.9 1.1 convolution_bitcast_fusion
  107.1 0.2 fusion.30
  107.3 0.2 fusion.29
  107.6 0.7 copy-done.2
  108.3 0.5 broadcast_multiply_fusion
  108.8 0.2 fusion.3
  109.1 0.2 fusion.4
  109.3 0.8 pad_maximum_fusion
  (24 shorter events, 0.5 us)
Async XLA Ops:
  7.2 3.4 %copy-start = (f32[4,8,16]{2,1,0:T(8,128)S(1)}, f32[4,8,16]{2,1,0:T(8,128)}, u32[]{:S(2)}) copy-start(f32[4,8,16]{2,1,0:T(8,128)} %param.14) | copy-start | bytes 6148
  7.2 0.7 copy-start.6
  7.2 2.2 %copy-start.3 = (s32[3,768]{1,0:T(4,128)S(1)}, s32[3,768]{1,0:T(4,128)}, u32[]{:S(2)}) copy-start(s32[3,768]{1,0:T(4,128)} %param.8) | copy-start | bytes 27652
  7.2 98.7 %all-reduce.2.cloned.1.call-start = ((), (), s32[]{:S(2)}) async-start(), calls=%async_computation | async-start | bytes 262144 | tf_op jit(solution)/shard_map/psum | solution.py:105
  8.6 0.8 copy-start.5
  9.5 0.7 copy-start.8
  10.3 0.7 copy-start.7
  11.2 1.0 copy-start.1
  13.7 0.8 copy-start.4
  107.3 0.9 copy-start.2
Sparse Core Ops, SparseCore 0:
  13.9 92.0 all-reduce.1
where the time goes:
time: 117 us
  waiting for transfers between devices  91.4 us (78%)
  between operations  14.2 us (12%)
  other arithmetic  4.1 us (4%)
  matrix products  3.75 us (3%)
  local copies, waits for them, and re-layouts  3.45 us (3%)
    psum x1, waiting for transfers between devices, on_device(): summed = lax.psum(local, 'ga')  91.3 us
    unnamed x19, local copies, waits for them, and re-layouts  3.43 us
  transfers between devices with their start and end apart: 1, of which 1 were waited for; matrix products, arithmetic and copies ran while one was open for 0% of the time, Pallas kernels for 0%

commit v1 on v0

--- a/solution.py
+++ b/solution.py
@@ -102,7 +102,7 @@
         )
 
     local = lax.fori_loop(0, blocks, first_pass, jnp.zeros((2, slots_all, bands), jnp.float32))
-    summed = lax.psum(local, "ga")
+    summed = jnp.sum(jax.lax.all_gather(local, "ga"), 0)
     shaped = summed.reshape(2, atoms, PROJ, summed.shape[2])
     weighted = jnp.einsum("aij,cajb->caib", coupling, shaped, precision=lax.Precision.HIGHEST)
     weighted = weighted.reshape(2, atoms * PROJ, summed.shape[2])

time: 117 us -> 72.3 us (0.62)
  the two profiles are of different devices: /device:TPU:8 before, /device:TPU:0 now
where the time goes in v1:
time: 72.3 us; the launch traced here: 71.9 us
  waiting for transfers between devices  44.2 us (61%)
  between operations  14.2 us (20%)
  other arithmetic  7.88 us (11%)
  matrix products  5.4 us (7%)
    all_gather x1, waiting for transfers between devices, on_device(): summed = jnp.sum(jax.lax.all_gather(local, 'ga'), 0)  44.2 us
    reduce_sum x1, other arithmetic, on_device(): summed = jnp.sum(jax.lax.all_gather(local, 'ga'), 0)  1.7 us
  transfers between devices with their start and end apart: 1, of which 1 were waited for; matrix products, arithmetic and copies ran while one was open for 0% of the time, Pallas kernels for 0%

profile of v1, /device:TPU:0, one launch (start us, length us, event | category | flops | bytes accessed | tf_op | source)
XLA Modules:
  0.0 71.9 jit_solution(4743672532773135019)
XLA Ops:
  7.2 0.0 all-gather.3.cloned.1.call-start
  7.2 0.8 %multiply_reduce_fusion = s32[16,768]{1,0:T(8,128)S(1)} fusion(s32[3,16]{1,0:T(4,128)} %param.13, s32[3,768]{1,0:T(4,128)} %param.8), kind=kLoop, calls=%fused_computation.28 | loop fusion | flops 61440 | bytes 58560 | tf_op jit(solution)/shard_map/while/body/eval_jaxpr/reduce_sum | solution.py:35
  8.1 0.8 %multiply_reduce_fusion.3 = f32[16]{0:T(128)S(1)} fusion(s32[3,16]{1,0:T(4,128)} %param.13, f32[3]{0:T(128)} %param.9), kind=kLoop, calls=%fused_computation.59 | loop fusion | flops 128 | bytes 268 | tf_op jit(solution)/shard_map/while/body/eval_jaxpr/reduce_sum | solution.py:36
  8.9 0.8 %multiply_reduce_fusion.2 = f32[768]{0:T(1024)S(1)} fusion(s32[3,768]{1,0:T(4,128)} %param.8, f32[3]{0:T(128)} %param.9), kind=kLoop, calls=%fused_computation.53 | loop fusion | flops 8448 | bytes 12300 | tf_op jit(solution)/shard_map/reduce_sum | solution.py:14
  9.7 0.8 %fusion.34 = f32[3,768]{1,0:T(4,128)S(1)} fusion(s32[3,768]{1,0:T(4,128)} %param.8, f32[768]{0:T(1024)S(1)} %add_sqrt_fusion, f32[3]{0:T(128)} %param.9), kind=kLoop, calls=%fused_computation.55 | loop fusion | flops 6912 | bytes 21516 | tf_op jit(solution)/shard_map/div | solution.py:18
  10.5 0.7 %fusion.35 = f32[16,8]{1,0:T(8,128)S(1)} fusion(s32[16]{0:T(128)} %param.12), kind=kLoop, calls=%fused_computation.57 | loop fusion | flops 256 | bytes 576 | tf_op jit(solution)/shard_map/while/body/eval_jaxpr/convert_element_type | solution.py:33
  11.2 0.3 fusion.39
  11.5 0.9 %fusion.32 = f32[16,8,16]{2,0,1:T(8,128)S(1)} fusion(f32[4,8,16]{2,1,0:T(8,128)S(1)} %copy-done, s32[16]{0:T(128)} %param.11), kind=kOutput, calls=%fused_computation.51 | convolution fusion | flops 98368 | bytes 10304 | tf_op jit(solution)/shard_map/while/body/eval_jaxpr/as,sjr->ajr/dot_general | solution.py:31
  12.4 0.6 fusion.8
  13.0 1.1 %fusion.13 = f32[128,128]{1,0:T(8,128)S(1)} fusion(bf16[128,768]{1,0:T(8,128)(2,1)S(1)} %get-tuple-element.51, bf16[2,128,768]{2,1,0:T(8,128)(2,1)} %param.10), kind=kOutput, calls=%fused_computation.22 | convolution fusion | flops 25165824 | bytes 458752 | tf_op jit(solution)/shard_map/while/body/eval_jaxpr/sg,bg->sb/dot_general | solution.py:53
  14.1 1.1 %fusion.9 = f32[128,128]{1,0:T(8,128)S(1)} fusion(bf16[128,768]{1,0:T(8,128)(2,1)S(1)} %get-tuple-element.51, bf16[2,128,768]{2,1,0:T(8,128)(2,1)} %param.10), kind=kOutput, calls=%fused_computation.18 | convolution fusion | flops 25165824 | bytes 458752 | tf_op jit(solution)/shard_map/while/body/eval_jaxpr/sg,bg->sb/dot_general | solution.py:56
  15.3 0.2 fusion.6
  15.5 0.2 fusion.5
  15.7 0.7 pad_maximum_fusion.1
  16.4 0.1 copy.24
  16.5 44.2 %all-gather.3.cloned.1.call-done = f32[32,128,128]{2,1,0:T(8,128)} async-done(((f32[2,128,128]{2,1,0:T(8,128)}), f32[32,128,128]{2,1,0:T(8,128)}) %all-gather.3.cloned.1.call-update) | async-done | bytes 2097168 | tf_op jit(solution)/shard_map/all_gather | solution.py:105
  60.8 1.7 %reduce_sum.60 = f32[2,128,128]{2,1,0:T(8,128)S(1)} reduce(f32[16,2,128,128]{3,2,1,0:T(8,128)} %bitcast.56, f32[]{:T(128)} %constant.62.clone.1), dimensions={0}, to_apply=%region_3.4 | reduce | flops 491520 | bytes 2228228 | tf_op jit(solution)/shard_map/reduce_sum | solution.py:105
  62.5 0.3 multiply_reduce_fusion.1
  62.7 0.2 fusion.28
  63.0 0.2 fusion.29
  63.2 0.2 fusion.4
  63.5 0.2 fusion.3
  63.7 0.5 broadcast_multiply_fusion
  64.2 0.8 %pad_maximum_fusion = bf16[2,128,768]{2,1,0:T(8,128)(2,1)} fusion(bf16[1,128,768]{2,1,0:T(8,128)(2,1)S(1)} %fusion.3, bf16[1,128,768]{2,1,0:T(8,128)(2,1)S(1)} %fusion.4), kind=kLoop, calls=%fused_computation.13 | loop fusion | flops 196608 | bytes 786432 | tf_op jit(solution)/shard_map/while/body/eval_jaxpr/stack | solution.py:69
  (11 shorter events, 0.1 us)
Async XLA Ops:
  7.2 4.3 %copy-start = (f32[4,8,16]{2,1,0:T(8,128)S(1)}, f32[4,8,16]{2,1,0:T(8,128)}, u32[]{:S(2)}) copy-start(f32[4,8,16]{2,1,0:T(8,128)} %param.14) | copy-start | bytes 6148
  7.2 8.1 %copy-start.1 = (bf16[2,128,768]{2,1,0:T(8,128)(2,1)S(1)}, bf16[2,128,768]{2,1,0:T(8,128)(2,1)}, u32[]{:S(2)}) copy-start(bf16[2,128,768]{2,1,0:T(8,128)(2,1)} %param.10) | copy-start | bytes 1179652
  7.2 9.2 %copy-start.2 = (f32[16,8,8]{0,2,1:T(8,128)S(1)}, f32[16,8,8]{0,2,1:T(8,128)}, u32[]{:S(2)}) copy-start(f32[16,8,8]{0,2,1:T(8,128)} %param.15) | copy-start | bytes 12292
  7.2 53.6 %all-gather.3.cloned.1.call-start = ((), (), s32[]{:S(2)}) async-start(), calls=%async_computation | async-start | bytes 2228224 | tf_op jit(solution)/shard_map/all_gather | solution.py:105
Sparse Core Ops, SparseCore 0:
  16.5 44.1 all-gather.2
